TPU v7x, 32 devices: a whole 2x2x4 slice. The times are simulated.
32 devices in a mesh: dp: 8 (over z, x), feat: 4 (over y, core).
Axes of the slice: x: 2, y: 2, z: 4, core: 2. Of those that a mesh axis runs over, the one named last changes fastest.
Arguments:
- activations: bfloat16 [2048, 8192], P('dp', 'feat'), may hold values from -6 to 6
- cotangent: bfloat16 [2048, 1024], P('dp'), may hold values from -0.13183594 to 0.13183594
- weight: float32 [8192, 1024], P('feat'), may hold values from -0.0625 to 0.0625
- stats_old: float32 [4, 8, 4, 256, 256], P('feat', 'dp'), as said below
- owners: int32 [32, 4], replicated, may hold values from 0 to 7, as said below
- next_acts: bfloat16 [2048, 8192], P('dp', 'feat'), may hold values from -6 to 6
Outputs:
- weight_new: float32 [8192, 1024], P('feat')
- stats_new: float32 [4, 8, 4, 256, 256], P('feat', 'dp')
- next_out: bfloat16 [2048, 1024], P('dp', 'feat')
Inputs may be any that keep to these rules, and one draw needn't show every extreme that they name: `owners`: blocks are grouped by the index of feat that holds their rows (8192 / (256 * 4) row blocks a group); in every group each dp index owns at most 4 blocks, and some dp index owns exactly 4. `stats_old`: every slot holds a symmetric positive definite matrix; slots that no block maps to are not read.
All inputs are finite; a program needn't handle non-finite values.
Results may differ from a plain program's by a relative error of at most 0.02.
Values may be sent and summed in bfloat16 or wider, within the bound.
A program may use at most 128 MiB of HBM per device.

v0:
```python
import jax
import jax.numpy as jnp
from jax import lax
from jax.sharding import PartitionSpec as P

ITERS = 6
decay_rate = 0.9
step_rate = 0.01


def from_root(x, axis, root):
    mine = lax.axis_index(axis) == root
    return lax.psum(jnp.where(mine, x, jnp.zeros_like(x)), axis)


def newton_root(stats):
    width = stats.shape[0]
    identity = jnp.eye(width, dtype=jnp.float32)
    norm_value = jnp.sqrt(jnp.sum(stats * stats) + 1e-06)
    matrix = stats / norm_value
    iterate = identity
    for counter in range(ITERS):
        factor = (5.0 * identity - matrix) / 4.0
        factor_low = factor.astype(jnp.bfloat16)
        iterate = jnp.dot(
            iterate.astype(jnp.bfloat16), factor_low, preferred_element_type=jnp.float32
        )
        if counter + 1 < ITERS:
            square = jnp.dot(factor_low, factor_low, preferred_element_type=jnp.float32).astype(
                jnp.bfloat16
            )
            fourth = jnp.dot(square, square, preferred_element_type=jnp.float32).astype(
                jnp.bfloat16
            )
            matrix = jnp.dot(
                fourth, matrix.astype(jnp.bfloat16), preferred_element_type=jnp.float32
            )
    return iterate * norm_value ** (-0.25)


def update_stats(grad_block, old_stats):
    gram = (
        jnp.dot(grad_block, grad_block.T, preferred_element_type=jnp.float32) / grad_block.shape[0]
    )
    return decay_rate * old_stats + (1.0 - decay_rate) * gram


def block_at(matrix, block_id, col_blocks, width):
    row_start = block_id // col_blocks * width
    col_start = block_id % col_blocks * width
    return lax.dynamic_slice(matrix, (row_start, col_start), (width, width))


def body(activations, cotangent, weight, stats_old, owners, next_acts):
    width = stats_old.shape[-1]
    slots = stats_old.shape[2]
    rows_dev, columns = weight.shape
    row_blocks = rows_dev // width
    col_blocks = columns // width
    block_count = row_blocks * col_blocks
    partial_grad = jnp.einsum(
        "td,tc->dc", activations, cotangent, preferred_element_type=jnp.float32
    )
    summed = lax.psum(partial_grad, "dp")
    grad_low = summed.astype(jnp.bfloat16)
    feat_index = lax.axis_index("feat")
    data_index = lax.axis_index("dp")
    own_list = lax.dynamic_slice_in_dim(owners, feat_index * row_blocks, row_blocks, 0).reshape(
        block_count
    )
    is_mine = (own_list == data_index).astype(jnp.int32)
    slot_of = jnp.cumsum(is_mine) - is_mine
    block_ids = jnp.arange(block_count, dtype=jnp.int32)
    slot_pick = jnp.clip(slot_of, 0, slots - 1)
    stats_list = []
    renewed_list = []
    chosen_list = []
    for position in range(slots):
        picked = (is_mine == 1) & (slot_of == position)
        alive = jnp.any(picked)
        chosen = jnp.sum(jnp.where(picked, block_ids, 0))
        grad_block = block_at(grad_low, chosen, col_blocks, width)
        renewed = update_stats(grad_block, stats_old[0, 0, position])
        stats_list.append(jnp.where(alive, renewed, 0.0))
        renewed_list.append(renewed)
        chosen_list.append(chosen)
    root_list = [newton_root(renewed) for renewed in renewed_list]
    new_list = []
    fresh_list = []
    for root_matrix, chosen in zip(root_list, chosen_list):
        grad_block = block_at(grad_low, chosen, col_blocks, width)
        weight_block = block_at(weight, chosen, col_blocks, width)
        update = jnp.dot(
            root_matrix.astype(jnp.bfloat16), grad_block, preferred_element_type=jnp.float32
        )
        fresh_list.append(weight_block - step_rate * update)
    candidates = jnp.stack(fresh_list)
    for position in range(block_count):
        sending = lax.dynamic_index_in_dim(candidates, slot_pick[position], 0, keepdims=False)
        new_list.append(
            from_root(sending.astype(jnp.bfloat16), "dp", own_list[position]).astype(sending.dtype)
        )
    new_blocks = jnp.stack(new_list)
    weight_new = (
        new_blocks.reshape(row_blocks, col_blocks, width, width)
        .transpose(0, 2, 1, 3)
        .reshape(rows_dev, columns)
    )
    stats_out = jnp.stack(stats_list)[None, None]
    partial_next = jnp.dot(
        next_acts, weight_new.astype(jnp.bfloat16), preferred_element_type=jnp.float32
    )
    next_out = lax.psum_scatter(
        partial_next.astype(jnp.bfloat16), "feat", scatter_dimension=1, tiled=True
    )
    return (weight_new, stats_out, next_out)


def solution(mesh):
    placed = (
        P("dp", "feat"),
        P("dp", None),
        P("feat", None),
        P("feat", "dp", None, None, None),
        P(),
        P("dp", "feat"),
    )
    return jax.shard_map(
        body,
        mesh=mesh,
        in_specs=placed,
        out_specs=(P("feat", None), P("feat", "dp", None, None, None), P("dp", "feat")),
        check_vma=False,
    )
```

profile of v0, /device:TPU:0, one launch (start us, length us, event | category | flops | bytes accessed | tf_op | source)
XLA Modules:
  0.0 700.2 jit_solution(15082206161460627291)
XLA Ops:
  7.2 0.8 constant_dynamic-slice_fusion
  8.5 0.7 fusion.355
  9.2 0.7 fusion.356
  9.9 0.6 select_reduce_fusion
  13.1 5.7 fusion.363
  18.9 328.1 %all-reduce.5 = bf16[2048,1024]{1,0:T(8,128)(2,1)} all-reduce(f32[2048,1024]{1,0:T(8,128)} %fusion.363), channel_id=1, replica_groups=mesh['dp'=8,'feat'=4] {'dp'}, use_global_device_ids=true, to_apply=%region_2.3 | all-reduce | flops 2097152 | bytes 12582912 | tf_op jit(solution)/shard_map/psum | solution.py:64
  347.0 1.8 multiply_reduce_fusion
  349.5 0.7 select_bitcast_fusion
  350.2 0.4 convolution_convert_fusion.13
  351.3 1.0 convolution_convert_fusion.12
  354.6 1.9 multiply_reduce_fusion.1
  357.1 0.7 select_bitcast_fusion.1
  357.8 0.4 convolution_convert_fusion.28
  358.5 0.4 convolution_convert_fusion.25
  358.9 1.0 convolution_convert_fusion.27
  360.0 0.6 select_reduce_fusion.2
  363.3 1.9 multiply_reduce_fusion.2
  365.8 0.6 select_bitcast_fusion.2
  367.6 1.0 convolution_convert_fusion.42
  370.9 1.8 multiply_reduce_fusion.3
  373.3 0.7 select_bitcast_fusion.3
  375.2 1.0 convolution_convert_fusion.57
  376.3 0.7 fusion.362
  378.3 0.7 fusion.361
  384.1 0.7 fusion.360
  386.3 0.7 fusion.359
  419.8 0.4 convolution_convert_fusion.7
  421.7 1.2 convolution_convert_fusion.6
  423.1 0.4 convolution_convert_fusion.22
  425.8 1.2 fusion.2
  427.4 1.2 fusion.6
  428.8 0.4 convolution_convert_fusion.37
  430.1 0.4 convolution_convert_fusion.31
  431.4 1.2 fusion.10
  435.5 1.2 fusion.14
  476.9 0.8 fusion.69
  477.7 1.0 fusion.78
  478.8 1.1 fusion.87
  479.8 1.1 fusion.96
  481.2 166.1 %all-reduce.4.cloned.1.call-done = (bf16[1,256,256]{2,1,0:T(8,128)(2,1)}, bf16[1,256,256]{2,1,0:T(8,128)(2,1)}, bf16[1,256,256]{2,1,0:T(8,128)(2,1)}, bf16[1,256...) async-done(((bf16[1,256,256]{2,1,0:T(8,128)(2,1)}, ...) | async-done | bytes 4194320 | tf_op jit(solution)/shard_map/psum | solution.py:13
  647.4 1.1 constant_dynamic-update-slice_fusion.31
  648.5 0.9 constant_dynamic-update-slice_fusion.30
  649.4 0.9 constant_dynamic-update-slice_fusion.29
  650.3 0.9 constant_dynamic-update-slice_fusion.28
  651.3 0.9 constant_dynamic-update-slice_fusion.27
  652.2 0.9 constant_dynamic-update-slice_fusion.26
  653.1 0.9 constant_dynamic-update-slice_fusion.25
  654.0 0.9 constant_dynamic-update-slice_fusion.24
  654.9 0.9 constant_dynamic-update-slice_fusion.23
  655.9 0.9 constant_dynamic-update-slice_fusion.22
  656.8 0.9 constant_dynamic-update-slice_fusion.21
  657.7 0.9 constant_dynamic-update-slice_fusion.20
  658.6 0.9 constant_dynamic-update-slice_fusion.19
  659.5 0.9 constant_dynamic-update-slice_fusion.18
  660.4 0.9 constant_dynamic-update-slice_fusion.17
  661.4 0.9 constant_dynamic-update-slice_fusion.16
  662.7 3.2 copy.15
  666.0 1.0 copy.18
  667.1 1.9 copy-done.2
  669.0 2.1 fusion
  671.2 1.0 maximum_bitcast_fusion
  672.2 6.6 reshape.195
  678.8 12.9 %reduce-scatter.2.cloned.1.call-done = bf16[256,256]{0,1:T(8,128)(2,1)} async-done(((bf16[256,1024]{0,1:T(8,128)(2,1)}), bf16[256,256]{0,1:T(8,128)(2,1)}) %reduce-scatter.2.cloned.1.call-update) | async-done | bytes 131088 | tf_op jit(solution)/shard_map/reduce_scatter | solution.py:113
  691.7 1.7 copy.16
  (116 shorter events, 13.0 us)
Async XLA Ops:
  7.2 6.0 copy-start
  7.2 640.1 %all-reduce.4.cloned.1.call-start = ((), (), s32[]{:S(2)}) async-start(), calls=%async_computation.2 | async-start | bytes 8388608 | tf_op jit(solution)/shard_map/psum | solution.py:13
  18.9 328.1 %copy-start.3 = (f32[1,1,4,256,256]{4,3,2,1,0:T(8,128)S(1)}, f32[1,1,4,256,256]{4,3,2,1,0:T(8,128)}, u32[]{:S(2)}) copy-start(f32[1,1,4,256,256]{4,3,2,1,0:T(8,128)} %param.9) | copy-start | bytes 3145732
  419.8 5.3 copy-start.21
  425.4 5.3 copy-start.22
  429.4 5.3 copy-start.23
  480.9 210.8 %reduce-scatter.2.cloned.1.call-start = ((), (), s32[]{:S(2)}) async-start(), calls=%async_computation.1 | async-start | bytes 655360 | tf_op jit(solution)/shard_map/reduce_scatter | solution.py:113
  647.3 15.0 %copy-start.19 = (bf16[1,256,256]{2,1,0:T(8,128)(2,1)S(1)}, bf16[1,256,256]{2,1,0:T(8,128)(2,1)}, u32[]{:S(2)}) copy-start(bf16[1,256,256]{2,1,0:T(8,128)(2,1)} %get-tuple-element.25) | copy-start | bytes 393220
  647.3 15.0 %copy-start.18 = (bf16[1,256,256]{2,1,0:T(8,128)(2,1)S(1)}, bf16[1,256,256]{2,1,0:T(8,128)(2,1)}, u32[]{:S(2)}) copy-start(bf16[1,256,256]{2,1,0:T(8,128)(2,1)} %get-tuple-element.26) | copy-start | bytes 393220
  647.3 15.0 %copy-start.17 = (bf16[1,256,256]{2,1,0:T(8,128)(2,1)S(1)}, bf16[1,256,256]{2,1,0:T(8,128)(2,1)}, u32[]{:S(2)}) copy-start(bf16[1,256,256]{2,1,0:T(8,128)(2,1)} %get-tuple-element.27) | copy-start | bytes 393220
  647.3 15.0 %copy-start.16 = (bf16[1,256,256]{2,1,0:T(8,128)(2,1)S(1)}, bf16[1,256,256]{2,1,0:T(8,128)(2,1)}, u32[]{:S(2)}) copy-start(bf16[1,256,256]{2,1,0:T(8,128)(2,1)} %get-tuple-element.28) | copy-start | bytes 393220
  647.3 15.1 %copy-start.15 = (bf16[1,256,256]{2,1,0:T(8,128)(2,1)S(1)}, bf16[1,256,256]{2,1,0:T(8,128)(2,1)}, u32[]{:S(2)}) copy-start(bf16[1,256,256]{2,1,0:T(8,128)(2,1)} %get-tuple-element.29) | copy-start | bytes 393220
  647.3 15.1 %copy-start.14 = (bf16[1,256,256]{2,1,0:T(8,128)(2,1)S(1)}, bf16[1,256,256]{2,1,0:T(8,128)(2,1)}, u32[]{:S(2)}) copy-start(bf16[1,256,256]{2,1,0:T(8,128)(2,1)} %get-tuple-element.30) | copy-start | bytes 393220
  647.3 15.1 %copy-start.13 = (bf16[1,256,256]{2,1,0:T(8,128)(2,1)S(1)}, bf16[1,256,256]{2,1,0:T(8,128)(2,1)}, u32[]{:S(2)}) copy-start(bf16[1,256,256]{2,1,0:T(8,128)(2,1)} %get-tuple-element.31) | copy-start | bytes 393220
  647.3 15.1 %copy-start.12 = (bf16[1,256,256]{2,1,0:T(8,128)(2,1)S(1)}, bf16[1,256,256]{2,1,0:T(8,128)(2,1)}, u32[]{:S(2)}) copy-start(bf16[1,256,256]{2,1,0:T(8,128)(2,1)} %get-tuple-element.32) | copy-start | bytes 393220
  647.4 15.2 %copy-start.11 = (bf16[1,256,256]{2,1,0:T(8,128)(2,1)S(1)}, bf16[1,256,256]{2,1,0:T(8,128)(2,1)}, u32[]{:S(2)}) copy-start(bf16[1,256,256]{2,1,0:T(8,128)(2,1)} %get-tuple-element.33) | copy-start | bytes 393220
  647.4 15.2 %copy-start.10 = (bf16[1,256,256]{2,1,0:T(8,128)(2,1)S(1)}, bf16[1,256,256]{2,1,0:T(8,128)(2,1)}, u32[]{:S(2)}) copy-start(bf16[1,256,256]{2,1,0:T(8,128)(2,1)} %get-tuple-element.34) | copy-start | bytes 393220
  647.4 15.2 %copy-start.9 = (bf16[1,256,256]{2,1,0:T(8,128)(2,1)S(1)}, bf16[1,256,256]{2,1,0:T(8,128)(2,1)}, u32[]{:S(2)}) copy-start(bf16[1,256,256]{2,1,0:T(8,128)(2,1)} %get-tuple-element.35) | copy-start | bytes 393220
  647.4 15.2 %copy-start.8 = (bf16[1,256,256]{2,1,0:T(8,128)(2,1)S(1)}, bf16[1,256,256]{2,1,0:T(8,128)(2,1)}, u32[]{:S(2)}) copy-start(bf16[1,256,256]{2,1,0:T(8,128)(2,1)} %get-tuple-element.36) | copy-start | bytes 393220
  647.4 15.2 %copy-start.7 = (bf16[1,256,256]{2,1,0:T(8,128)(2,1)S(1)}, bf16[1,256,256]{2,1,0:T(8,128)(2,1)}, u32[]{:S(2)}) copy-start(bf16[1,256,256]{2,1,0:T(8,128)(2,1)} %get-tuple-element.37) | copy-start | bytes 393220
  647.4 15.2 %copy-start.6 = (bf16[1,256,256]{2,1,0:T(8,128)(2,1)S(1)}, bf16[1,256,256]{2,1,0:T(8,128)(2,1)}, u32[]{:S(2)}) copy-start(bf16[1,256,256]{2,1,0:T(8,128)(2,1)} %get-tuple-element.38) | copy-start | bytes 393220
  647.4 15.3 %copy-start.5 = (bf16[1,256,256]{2,1,0:T(8,128)(2,1)S(1)}, bf16[1,256,256]{2,1,0:T(8,128)(2,1)}, u32[]{:S(2)}) copy-start(bf16[1,256,256]{2,1,0:T(8,128)(2,1)} %get-tuple-element.39) | copy-start | bytes 393220
  647.4 15.3 %copy-start.4 = (bf16[1,256,256]{2,1,0:T(8,128)(2,1)S(1)}, bf16[1,256,256]{2,1,0:T(8,128)(2,1)}, u32[]{:S(2)}) copy-start(bf16[1,256,256]{2,1,0:T(8,128)(2,1)} %get-tuple-element.40) | copy-start | bytes 393220
  666.0 3.0 copy-start.20
  667.0 1.9 copy-start.2
  671.1 22.2 %copy-start.1 = (bf16[256,2048]{1,0:T(8,128)(2,1)S(1)}, bf16[256,2048]{1,0:T(8,128)(2,1)}, u32[]{:S(2)}) copy-start(bf16[256,2048]{1,0:T(8,128)(2,1)} %param.6) | copy-start | bytes 3145732
Sparse Core Ops, SparseCore 0:
  481.0 166.2 all-reduce.3
  671.3 20.4 reduce-scatter.1
where the time goes:
time: 702 us; the launch traced here: 700 us
  blocking collectives  328 us (47%)
  waiting for transfers between devices  179 us (25%)
  between operations  108 us (15%)
  matrix products  40.3 us (6%)
  local copies, waits for them, and re-layouts  27 us (4%)
  other arithmetic  17.4 us (2%)
    psum x1, blocking collectives, body(): summed = lax.psum(partial_grad, 'dp')  328 us
    psum x1, waiting for transfers between devices, from_root(): return lax.psum(jnp.where(mine, x, jnp.zeros_like(x)), axis)  166 us
    unnamed x82, local copies, waits for them, and re-layouts  19.8 us
  transfers between devices with their start and end apart: 2, of which 2 were waited for; matrix products, arithmetic and copies ran while one was open for 1% of the time, Pallas kernels for 0%

commit v1 on v0

--- a/solution.py
+++ b/solution.py
@@ -8,9 +8,13 @@
 step_rate = 0.01
 
 
+def tell_islands(view, mesh_name):
+    return jnp.sum(lax.all_gather(view, mesh_name), axis=0)
+
+
 def from_root(x, axis, root):
     mine = lax.axis_index(axis) == root
-    return lax.psum(jnp.where(mine, x, jnp.zeros_like(x)), axis)
+    return tell_islands(jnp.where(mine, x, jnp.zeros_like(x)), axis)
 
 
 def newton_root(stats):

time: 702 us -> 1780 us (2.54)
  waiting for transfers between devices: 179 us -> 1190 us
  other arithmetic: 17.4 us -> 54.7 us
  local copies, waits for them, and re-layouts: 27 us -> 47.5 us
    all_gather x0 -> x32, waiting for transfers between devices: none -> 1160 us  [tell_islands(): return jnp.sum(lax.all_gather(view, mesh_name), axis=0)]
    psum x1 -> x0, waiting for transfers between devices: 166 us -> none  [from_root(): return lax.psum(jnp.where(mine, x, jnp.zeros_like(x)), axis)]
    reduce_sum x0 -> x32, other arithmetic: none -> 43.9 us  [tell_islands(): return jnp.sum(lax.all_gather(view, mesh_name), axis=0)]
  transfers between devices with their start and end apart: 2 -> 33, of which waited for: 2 -> 31; matrix products, arithmetic and copies ran while one was open for 1% -> 4% of each run, Pallas kernels for 0% -> 0%
where the time goes in v1:
time: 1780 us; the launch traced here: 1770 us
  waiting for transfers between devices  1190 us (67%)
  blocking collectives  328 us (18%)
  between operations  110 us (6%)
  other arithmetic  54.7 us (3%)
  local copies, waits for them, and re-layouts  47.5 us (3%)
  matrix products  43.7 us (2%)
    all_gather x32, waiting for transfers between devices, tell_islands(): return jnp.sum(lax.all_gather(view, mesh_name), axis=0)  1160 us
    psum x1, blocking collectives, body(): summed = lax.psum(partial_grad, 'dp')  328 us
    reduce_sum x32, other arithmetic, tell_islands(): return jnp.sum(lax.all_gather(view, mesh_name), axis=0)  43.9 us
  transfers between devices with their start and end apart: 33, of which 31 were waited for; matrix products, arithmetic and copies ran while one was open for 4% of the time, Pallas kernels for 0%

profile of v1, /device:TPU:0, one launch (start us, length us, event | category | flops | bytes accessed | tf_op | source)
XLA Modules:
  0.0 1773.1 jit_solution(9728453864608357082)
XLA Ops:
  13.1 5.7 fusion.363
  18.9 328.1 %all-reduce.1 = bf16[2048,1024]{1,0:T(8,128)(2,1)} all-reduce(f32[2048,1024]{1,0:T(8,128)} %fusion.363), channel_id=1, replica_groups=mesh['dp'=8,'feat'=4] {'dp'}, use_global_device_ids=true, to_apply=%region_2.3 | all-reduce | flops 2097152 | bytes 12582912 | tf_op jit(solution)/shard_map/psum | solution.py:68
  347.0 1.8 multiply_reduce_fusion
  355.1 1.9 multiply_reduce_fusion.1
  363.9 1.9 multiply_reduce_fusion.2
  372.1 1.9 multiply_reduce_fusion.3
  390.8 1.9 convolution_convert_fusion.21
  505.3 1.4 reduce_sum.464
  507.4 1.4 reduce_sum.465
  509.4 24.8 %all-gather.37.cloned.1.call-done = bf16[8,256,256]{2,1,0:T(8,128)(2,1)} async-done(((bf16[1,256,256]{2,1,0:T(8,128)(2,1)}), bf16[8,256,256]{2,1,0:T(8,128)(2,1)}) %all-gather.37.cloned.1.call-update) | async-done | bytes 1048592 | tf_op jit(solution)/shard_map/all_gather | solution.py:12
  534.2 1.4 reduce_sum.466
  536.3 39.5 %all-gather.39.cloned.1.call-done = bf16[8,256,256]{2,1,0:T(8,128)(2,1)} async-done(((bf16[1,256,256]{2,1,0:T(8,128)(2,1)}), bf16[8,256,256]{2,1,0:T(8,128)(2,1)}) %all-gather.39.cloned.1.call-update) | async-done | bytes 1048592 | tf_op jit(solution)/shard_map/all_gather | solution.py:12
  575.8 1.4 reduce_sum.467
  577.8 39.5 %all-gather.41.cloned.1.call-done = bf16[8,256,256]{2,1,0:T(8,128)(2,1)} async-done(((bf16[1,256,256]{2,1,0:T(8,128)(2,1)}), bf16[8,256,256]{2,1,0:T(8,128)(2,1)}) %all-gather.41.cloned.1.call-update) | async-done | bytes 1048592 | tf_op jit(solution)/shard_map/all_gather | solution.py:12
  617.4 1.4 reduce_sum.468
  619.4 39.0 %all-gather.43.cloned.1.call-done = bf16[8,256,256]{2,1,0:T(8,128)(2,1)} async-done(((bf16[1,256,256]{2,1,0:T(8,128)(2,1)}), bf16[8,256,256]{2,1,0:T(8,128)(2,1)}) %all-gather.43.cloned.1.call-update) | async-done | bytes 1048592 | tf_op jit(solution)/shard_map/all_gather | solution.py:12
  658.4 1.4 reduce_sum.469
  660.4 39.1 %all-gather.45.cloned.1.call-done = bf16[8,256,256]{2,1,0:T(8,128)(2,1)} async-done(((bf16[1,256,256]{2,1,0:T(8,128)(2,1)}), bf16[8,256,256]{2,1,0:T(8,128)(2,1)}) %all-gather.45.cloned.1.call-update) | async-done | bytes 1048592 | tf_op jit(solution)/shard_map/all_gather | solution.py:12
  699.5 1.4 reduce_sum.470
  701.5 39.1 %all-gather.47.cloned.1.call-done = bf16[8,256,256]{2,1,0:T(8,128)(2,1)} async-done(((bf16[1,256,256]{2,1,0:T(8,128)(2,1)}), bf16[8,256,256]{2,1,0:T(8,128)(2,1)}) %all-gather.47.cloned.1.call-update) | async-done | bytes 1048592 | tf_op jit(solution)/shard_map/all_gather | solution.py:12
  740.6 1.4 reduce_sum.471
  742.7 39.1 %all-gather.49.cloned.1.call-done = bf16[8,256,256]{2,1,0:T(8,128)(2,1)} async-done(((bf16[1,256,256]{2,1,0:T(8,128)(2,1)}), bf16[8,256,256]{2,1,0:T(8,128)(2,1)}) %all-gather.49.cloned.1.call-update) | async-done | bytes 1048592 | tf_op jit(solution)/shard_map/all_gather | solution.py:12
  781.8 1.4 reduce_sum.472
  783.8 39.0 %all-gather.51.cloned.1.call-done = bf16[8,256,256]{2,1,0:T(8,128)(2,1)} async-done(((bf16[1,256,256]{2,1,0:T(8,128)(2,1)}), bf16[8,256,256]{2,1,0:T(8,128)(2,1)}) %all-gather.51.cloned.1.call-update) | async-done | bytes 1048592 | tf_op jit(solution)/shard_map/all_gather | solution.py:12
  822.8 1.4 reduce_sum.473
  824.8 39.1 %all-gather.53.cloned.1.call-done = bf16[8,256,256]{2,1,0:T(8,128)(2,1)} async-done(((bf16[1,256,256]{2,1,0:T(8,128)(2,1)}), bf16[8,256,256]{2,1,0:T(8,128)(2,1)}) %all-gather.53.cloned.1.call-update) | async-done | bytes 1048592 | tf_op jit(solution)/shard_map/all_gather | solution.py:12
  863.9 1.4 reduce_sum.474
  866.0 39.0 %all-gather.55.cloned.1.call-done = bf16[8,256,256]{2,1,0:T(8,128)(2,1)} async-done(((bf16[1,256,256]{2,1,0:T(8,128)(2,1)}), bf16[8,256,256]{2,1,0:T(8,128)(2,1)}) %all-gather.55.cloned.1.call-update) | async-done | bytes 1048592 | tf_op jit(solution)/shard_map/all_gather | solution.py:12
  904.9 1.4 reduce_sum.475
  907.0 39.1 %all-gather.57.cloned.1.call-done = bf16[8,256,256]{2,1,0:T(8,128)(2,1)} async-done(((bf16[1,256,256]{2,1,0:T(8,128)(2,1)}), bf16[8,256,256]{2,1,0:T(8,128)(2,1)}) %all-gather.57.cloned.1.call-update) | async-done | bytes 1048592 | tf_op jit(solution)/shard_map/all_gather | solution.py:12
  946.1 1.4 reduce_sum.476
  948.1 39.0 %all-gather.59.cloned.1.call-done = bf16[8,256,256]{2,1,0:T(8,128)(2,1)} async-done(((bf16[1,256,256]{2,1,0:T(8,128)(2,1)}), bf16[8,256,256]{2,1,0:T(8,128)(2,1)}) %all-gather.59.cloned.1.call-update) | async-done | bytes 1048592 | tf_op jit(solution)/shard_map/all_gather | solution.py:12
  987.1 1.4 reduce_sum.477
  989.1 39.0 %all-gather.61.cloned.1.call-done = bf16[8,256,256]{2,1,0:T(8,128)(2,1)} async-done(((bf16[1,256,256]{2,1,0:T(8,128)(2,1)}), bf16[8,256,256]{2,1,0:T(8,128)(2,1)}) %all-gather.61.cloned.1.call-update) | async-done | bytes 1048592 | tf_op jit(solution)/shard_map/all_gather | solution.py:12
  1028.1 1.4 reduce_sum.478
  1030.1 39.0 %all-gather.63.cloned.1.call-done = bf16[8,256,256]{2,1,0:T(8,128)(2,1)} async-done(((bf16[1,256,256]{2,1,0:T(8,128)(2,1)}), bf16[8,256,256]{2,1,0:T(8,128)(2,1)}) %all-gather.63.cloned.1.call-update) | async-done | bytes 1048592 | tf_op jit(solution)/shard_map/all_gather | solution.py:12
  1069.1 1.4 reduce_sum.479
  1071.1 39.0 %all-gather.65.cloned.1.call-done = bf16[8,256,256]{2,1,0:T(8,128)(2,1)} async-done(((bf16[1,256,256]{2,1,0:T(8,128)(2,1)}), bf16[8,256,256]{2,1,0:T(8,128)(2,1)}) %all-gather.65.cloned.1.call-update) | async-done | bytes 1048592 | tf_op jit(solution)/shard_map/all_gather | solution.py:12
  1110.1 1.4 reduce_sum.480
  1112.1 39.0 %all-gather.67.cloned.1.call-done = bf16[8,256,256]{2,1,0:T(8,128)(2,1)} async-done(((bf16[1,256,256]{2,1,0:T(8,128)(2,1)}), bf16[8,256,256]{2,1,0:T(8,128)(2,1)}) %all-gather.67.cloned.1.call-update) | async-done | bytes 1048592 | tf_op jit(solution)/shard_map/all_gather | solution.py:12
  1151.1 1.4 reduce_sum.481
  1153.1 39.1 %all-gather.69.cloned.1.call-done = bf16[8,256,256]{2,1,0:T(8,128)(2,1)} async-done(((bf16[1,256,256]{2,1,0:T(8,128)(2,1)}), bf16[8,256,256]{2,1,0:T(8,128)(2,1)}) %all-gather.69.cloned.1.call-update) | async-done | bytes 1048592 | tf_op jit(solution)/shard_map/all_gather | solution.py:12
  1192.2 1.4 reduce_sum.482
  1194.3 39.0 %all-gather.71.cloned.1.call-done = bf16[8,256,256]{2,1,0:T(8,128)(2,1)} async-done(((bf16[1,256,256]{2,1,0:T(8,128)(2,1)}), bf16[8,256,256]{2,1,0:T(8,128)(2,1)}) %all-gather.71.cloned.1.call-update) | async-done | bytes 1048592 | tf_op jit(solution)/shard_map/all_gather | solution.py:12
  1235.3 39.1 %all-gather.73.cloned.1.call-done = bf16[8,256,256]{2,1,0:T(8,128)(2,1)} async-done(((bf16[1,256,256]{2,1,0:T(8,128)(2,1)}), bf16[8,256,256]{2,1,0:T(8,128)(2,1)}) %all-gather.73.cloned.1.call-update) | async-done | bytes 1048592 | tf_op jit(solution)/shard_map/all_gather | solution.py:12
  1276.4 39.1 %all-gather.75.cloned.1.call-done = bf16[8,256,256]{2,1,0:T(8,128)(2,1)} async-done(((bf16[1,256,256]{2,1,0:T(8,128)(2,1)}), bf16[8,256,256]{2,1,0:T(8,128)(2,1)}) %all-gather.75.cloned.1.call-update) | async-done | bytes 1048592 | tf_op jit(solution)/shard_map/all_gather | solution.py:12
  1317.6 39.1 %all-gather.77.cloned.1.call-done = bf16[8,256,256]{2,1,0:T(8,128)(2,1)} async-done(((bf16[1,256,256]{2,1,0:T(8,128)(2,1)}), bf16[8,256,256]{2,1,0:T(8,128)(2,1)}) %all-gather.77.cloned.1.call-update) | async-done | bytes 1048592 | tf_op jit(solution)/shard_map/all_gather | solution.py:12
  1358.7 39.0 %all-gather.79.cloned.1.call-done = bf16[8,256,256]{2,1,0:T(8,128)(2,1)} async-done(((bf16[1,256,256]{2,1,0:T(8,128)(2,1)}), bf16[8,256,256]{2,1,0:T(8,128)(2,1)}) %all-gather.79.cloned.1.call-update) | async-done | bytes 1048592 | tf_op jit(solution)/shard_map/all_gather | solution.py:12
  1399.1 39.8 %all-gather.81.cloned.1.call-done = bf16[8,256,256]{2,1,0:T(8,128)(2,1)} async-done(((bf16[1,256,256]{2,1,0:T(8,128)(2,1)}), bf16[8,256,256]{2,1,0:T(8,128)(2,1)}) %all-gather.81.cloned.1.call-update) | async-done | bytes 1048592 | tf_op jit(solution)/shard_map/all_gather | solution.py:12
  1440.2 39.6 %all-gather.83.cloned.1.call-done = bf16[8,256,256]{2,1,0:T(8,128)(2,1)} async-done(((bf16[1,256,256]{2,1,0:T(8,128)(2,1)}), bf16[8,256,256]{2,1,0:T(8,128)(2,1)}) %all-gather.83.cloned.1.call-update) | async-done | bytes 1048592 | tf_op jit(solution)/shard_map/all_gather | solution.py:12
  1481.2 39.6 %all-gather.85.cloned.1.call-done = bf16[8,256,256]{2,1,0:T(8,128)(2,1)} async-done(((bf16[1,256,256]{2,1,0:T(8,128)(2,1)}), bf16[8,256,256]{2,1,0:T(8,128)(2,1)}) %all-gather.85.cloned.1.call-update) | async-done | bytes 1048592 | tf_op jit(solution)/shard_map/all_gather | solution.py:12
  1520.8 1.4 reduce_sum.490
  1522.2 39.8 %all-gather.87.cloned.1.call-done = bf16[8,256,256]{2,1,0:T(8,128)(2,1)} async-done(((bf16[1,256,256]{2,1,0:T(8,128)(2,1)}), bf16[8,256,256]{2,1,0:T(8,128)(2,1)}) %all-gather.87.cloned.1.call-update) | async-done | bytes 1048592 | tf_op jit(solution)/shard_map/all_gather | solution.py:12
  1563.3 39.8 %all-gather.89.cloned.1.call-done = bf16[8,256,256]{2,1,0:T(8,128)(2,1)} async-done(((bf16[1,256,256]{2,1,0:T(8,128)(2,1)}), bf16[8,256,256]{2,1,0:T(8,128)(2,1)}) %all-gather.89.cloned.1.call-update) | async-done | bytes 1048592 | tf_op jit(solution)/shard_map/all_gather | solution.py:12
  1604.5 39.6 %all-gather.91.cloned.1.call-done = bf16[8,256,256]{2,1,0:T(8,128)(2,1)} async-done(((bf16[1,256,256]{2,1,0:T(8,128)(2,1)}), bf16[8,256,256]{2,1,0:T(8,128)(2,1)}) %all-gather.91.cloned.1.call-update) | async-done | bytes 1048592 | tf_op jit(solution)/shard_map/all_gather | solution.py:12
  1645.5 39.8 %all-gather.93.cloned.1.call-done = bf16[8,256,256]{2,1,0:T(8,128)(2,1)} async-done(((bf16[1,256,256]{2,1,0:T(8,128)(2,1)}), bf16[8,256,256]{2,1,0:T(8,128)(2,1)}) %all-gather.93.cloned.1.call-update) | async-done | bytes 1048592 | tf_op jit(solution)/shard_map/all_gather | solution.py:12
  1692.0 34.5 %all-gather.95.cloned.1.call-done = bf16[8,256,256]{2,1,0:T(8,128)(2,1)} async-done(((bf16[1,256,256]{2,1,0:T(8,128)(2,1)}), bf16[8,256,256]{2,1,0:T(8,128)(2,1)}) %all-gather.95.cloned.1.call-update) | async-done | bytes 1048592 | tf_op jit(solution)/shard_map/all_gather | solution.py:12
  1728.5 7.8 copy.22
  1736.3 3.8 copy.26
  1740.1 1.9 copy-done.2
  1742.0 2.1 fusion
  1745.2 6.9 copy.23
  1752.0 12.6 reduce-scatter.2.cloned.1.call-done
  1764.6 1.7 copy.24
  (205 shorter events, 97.9 us)
Async XLA Ops:
  7.2 6.0 copy-start
  7.2 498.2 %all-gather.33.cloned.1.call-start = ((), (), s32[]{:S(2)}) async-start(), calls=%async_computation.1 | async-start | bytes 1179648 | tf_op jit(solution)/shard_map/all_gather | solution.py:12
  18.9 328.1 %copy-start.3 = (f32[1,1,4,256,256]{4,3,2,1,0:T(8,128)S(1)}, f32[1,1,4,256,256]{4,3,2,1,0:T(8,128)}, u32[]{:S(2)}) copy-start(f32[1,1,4,256,256]{4,3,2,1,0:T(8,128)} %param.9) | copy-start | bytes 3145732
  397.6 6.3 copy-start.5
  413.1 94.3 %all-gather.35.cloned.1.call-start = ((), (), s32[]{:S(2)}) async-start(), calls=%async_computation.2 | async-start | bytes 1179648 | tf_op jit(solution)/shard_map/all_gather | solution.py:12
  413.9 120.3 %all-gather.37.cloned.1.call-start = ((), (), s32[]{:S(2)}) async-start(), calls=%async_computation.3 | async-start | bytes 1179648 | tf_op jit(solution)/shard_map/all_gather | solution.py:12
  414.6 161.2 %all-gather.39.cloned.1.call-start = ((), (), s32[]{:S(2)}) async-start(), calls=%async_computation.4 | async-start | bytes 1179648 | tf_op jit(solution)/shard_map/all_gather | solution.py:12
  415.2 202.2 %all-gather.41.cloned.1.call-start = ((), (), s32[]{:S(2)}) async-start(), calls=%async_computation.5 | async-start | bytes 1179648 | tf_op jit(solution)/shard_map/all_gather | solution.py:12
  415.8 242.6 %all-gather.43.cloned.1.call-start = ((), (), s32[]{:S(2)}) async-start(), calls=%async_computation.6 | async-start | bytes 1179648 | tf_op jit(solution)/shard_map/all_gather | solution.py:12
  441.0 258.5 %all-gather.45.cloned.1.call-start = ((), (), s32[]{:S(2)}) async-start(), calls=%async_computation.7 | async-start | bytes 1179648 | tf_op jit(solution)/shard_map/all_gather | solution.py:12
  441.8 298.9 %all-gather.47.cloned.1.call-start = ((), (), s32[]{:S(2)}) async-start(), calls=%async_computation.8 | async-start | bytes 1179648 | tf_op jit(solution)/shard_map/all_gather | solution.py:12
  442.5 339.3 %all-gather.49.cloned.1.call-start = ((), (), s32[]{:S(2)}) async-start(), calls=%async_computation.9 | async-start | bytes 1179648 | tf_op jit(solution)/shard_map/all_gather | solution.py:12
  443.2 379.6 %all-gather.51.cloned.1.call-start = ((), (), s32[]{:S(2)}) async-start(), calls=%async_computation.10 | async-start | bytes 1179648 | tf_op jit(solution)/shard_map/all_gather | solution.py:12
  443.8 420.1 %all-gather.53.cloned.1.call-start = ((), (), s32[]{:S(2)}) async-start(), calls=%async_computation.11 | async-start | bytes 1179648 | tf_op jit(solution)/shard_map/all_gather | solution.py:12
  444.6 460.4 %all-gather.55.cloned.1.call-start = ((), (), s32[]{:S(2)}) async-start(), calls=%async_computation.12 | async-start | bytes 1179648 | tf_op jit(solution)/shard_map/all_gather | solution.py:12
  445.1 501.0 %all-gather.57.cloned.1.call-start = ((), (), s32[]{:S(2)}) async-start(), calls=%async_computation.13 | async-start | bytes 1179648 | tf_op jit(solution)/shard_map/all_gather | solution.py:12
  445.9 541.2 %all-gather.59.cloned.1.call-start = ((), (), s32[]{:S(2)}) async-start(), calls=%async_computation.14 | async-start | bytes 1179648 | tf_op jit(solution)/shard_map/all_gather | solution.py:12
  446.5 581.6 %all-gather.61.cloned.1.call-start = ((), (), s32[]{:S(2)}) async-start(), calls=%async_computation.15 | async-start | bytes 1179648 | tf_op jit(solution)/shard_map/all_gather | solution.py:12
  470.3 598.8 %all-gather.63.cloned.1.call-start = ((), (), s32[]{:S(2)}) async-start(), calls=%async_computation.16 | async-start | bytes 1179648 | tf_op jit(solution)/shard_map/all_gather | solution.py:12
  470.9 639.2 %all-gather.65.cloned.1.call-start = ((), (), s32[]{:S(2)}) async-start(), calls=%async_computation.17 | async-start | bytes 1179648 | tf_op jit(solution)/shard_map/all_gather | solution.py:12
  471.5 679.6 %all-gather.67.cloned.1.call-start = ((), (), s32[]{:S(2)}) async-start(), calls=%async_computation.18 | async-start | bytes 1179648 | tf_op jit(solution)/shard_map/all_gather | solution.py:12
  472.1 720.2 %all-gather.69.cloned.1.call-start = ((), (), s32[]{:S(2)}) async-start(), calls=%async_computation.19 | async-start | bytes 1179648 | tf_op jit(solution)/shard_map/all_gather | solution.py:12
  472.8 760.4 %all-gather.71.cloned.1.call-start = ((), (), s32[]{:S(2)}) async-start(), calls=%async_computation.20 | async-start | bytes 1179648 | tf_op jit(solution)/shard_map/all_gather | solution.py:12
  473.4 801.0 %all-gather.73.cloned.1.call-start = ((), (), s32[]{:S(2)}) async-start(), calls=%async_computation.21 | async-start | bytes 1179648 | tf_op jit(solution)/shard_map/all_gather | solution.py:12
  474.1 841.4 %all-gather.75.cloned.1.call-start = ((), (), s32[]{:S(2)}) async-start(), calls=%async_computation.22 | async-start | bytes 1179648 | tf_op jit(solution)/shard_map/all_gather | solution.py:12
  474.9 881.8 %all-gather.77.cloned.1.call-start = ((), (), s32[]{:S(2)}) async-start(), calls=%async_computation.23 | async-start | bytes 1179648 | tf_op jit(solution)/shard_map/all_gather | solution.py:12
  475.6 922.1 %all-gather.79.cloned.1.call-start = ((), (), s32[]{:S(2)}) async-start(), calls=%async_computation.24 | async-start | bytes 1179648 | tf_op jit(solution)/shard_map/all_gather | solution.py:12
  499.8 939.0 %all-gather.81.cloned.1.call-start = ((), (), s32[]{:S(2)}) async-start(), calls=%async_computation.25 | async-start | bytes 1179648 | tf_op jit(solution)/shard_map/all_gather | solution.py:12
  500.6 979.3 %all-gather.83.cloned.1.call-start = ((), (), s32[]{:S(2)}) async-start(), calls=%async_computation.26 | async-start | bytes 1179648 | tf_op jit(solution)/shard_map/all_gather | solution.py:12
  501.1 1019.7 %all-gather.85.cloned.1.call-start = ((), (), s32[]{:S(2)}) async-start(), calls=%async_computation.27 | async-start | bytes 1179648 | tf_op jit(solution)/shard_map/all_gather | solution.py:12
  501.7 1060.2 %all-gather.87.cloned.1.call-start = ((), (), s32[]{:S(2)}) async-start(), calls=%async_computation.28 | async-start | bytes 1179648 | tf_op jit(solution)/shard_map/all_gather | solution.py:12
  502.5 1100.6 %all-gather.89.cloned.1.call-start = ((), (), s32[]{:S(2)}) async-start(), calls=%async_computation.29 | async-start | bytes 1179648 | tf_op jit(solution)/shard_map/all_gather | solution.py:12
  503.2 1140.9 %all-gather.91.cloned.1.call-start = ((), (), s32[]{:S(2)}) async-start(), calls=%async_computation.30 | async-start | bytes 1179648 | tf_op jit(solution)/shard_map/all_gather | solution.py:12
  503.8 1181.5 %all-gather.93.cloned.1.call-start = ((), (), s32[]{:S(2)}) async-start(), calls=%async_computation.31 | async-start | bytes 1179648 | tf_op jit(solution)/shard_map/all_gather | solution.py:12
  504.5 1221.9 %all-gather.95.cloned.1.call-start = ((), (), s32[]{:S(2)}) async-start(), calls=%async_computation.32 | async-start | bytes 1179648 | tf_op jit(solution)/shard_map/all_gather | solution.py:12
  505.3 1259.4 %reduce-scatter.2.cloned.1.call-start = ((), (), s32[]{:S(2)}) async-start(), calls=%async_computation.33 | async-start | bytes 655360 | tf_op jit(solution)/shard_map/reduce_scatter | solution.py:117
  1736.3 5.7 copy-start.4
  1740.1 1.9 copy-start.2
  1744.1 22.2 %copy-start.1 = (bf16[256,2048]{1,0:T(8,128)(2,1)S(1)}, bf16[256,2048]{1,0:T(8,128)(2,1)}, u32[]{:S(2)}) copy-start(bf16[256,2048]{1,0:T(8,128)(2,1)} %param.6) | copy-start | bytes 3145732
Sparse Core Ops, SparseCore 0:
  413.2 38.6 all-gather.32
  454.0 39.0 all-gather.34
  495.2 38.9 all-gather.36
  536.8 38.9 all-gather.38
  578.3 38.9 all-gather.40
  619.3 38.9 all-gather.42
  660.5 38.9 all-gather.44
  701.6 38.9 all-gather.46
  742.8 38.9 all-gather.48
  783.8 38.9 all-gather.50
  824.9 38.9 all-gather.52
  865.9 38.9 all-gather.54
  907.1 38.9 all-gather.56
  948.1 38.9 all-gather.58
  989.1 38.9 all-gather.60
  1030.1 38.9 all-gather.62
  1071.1 38.9 all-gather.64
  1112.1 38.9 all-gather.66
  1153.2 38.9 all-gather.68
  1194.2 38.9 all-gather.70
  1235.4 38.9 all-gather.72
  1276.5 38.9 all-gather.74
  1317.7 38.9 all-gather.76
  1358.7 38.9 all-gather.78
  1399.8 38.9 all-gather.80
  1440.8 38.9 all-gather.82
  1481.8 38.9 all-gather.84
  1522.9 38.9 all-gather.86
  1564.1 38.9 all-gather.88
  1605.1 38.9 all-gather.90
  1646.2 38.9 all-gather.92
  1687.4 38.9 all-gather.94
  1744.2 20.3 reduce-scatter.1
